TPU v7x, 32 devices: a whole 2x2x4 slice. The times are simulated.
32 devices in a mesh: freq: 8 (over y, x, core), base: 4 (over z).
Axes of the slice: x: 2, y: 2, z: 4, core: 2. Of those that a mesh axis runs over, the one named last changes fastest.
Arguments:
- visibility: float32 [2, 16, 2048], P(None, 'freq', 'base'), may hold values from -6 to 6
- tile_of: int32 [16, 2048, 1], P('freq', 'base'), may hold values from 0 to 3; in each aligned block of 512 rows (0 to 511, 512 to 1023, ..., all dimensions but the last counted through in order) at most 256 rows name the same one
- u_within: int32 [16, 2048], P('freq', 'base'), may hold values from 0 to 255
- v_cell: int32 [16, 2048], P('freq', 'base'), may hold values from 0 to 1016
- kernel_index: int32 [2, 16, 2048], P(None, 'freq', 'base'), may hold values from 0 to 127
- kernel: float32 [128, 8], replicated, may hold values from 0.1 to 1
- live_count: int32 [16, 4], P('freq', 'base'), may hold values from 64 to 512, as said below
- bin_map: int32 [1024, 1024], P('base'), may hold values from 0 to 511, as said below
Outputs:
- power_map: float32 [1024, 1024], P('freq', 'base')
- spectrum: float32 [512], replicated
Inputs may be any that keep to these rules, and one draw needn't show every extreme that they name: `tile_of`: among the visibilities of one channel on one device, at most 256 name the same tile, and in some device's visibilities a tile is named by exactly 256. `live_count`: the first device along base holds 512 used slots in every channel; the used slots of a device are its first ones. `bin_map`: every bin number occurs.
All inputs are finite; a program needn't handle non-finite values.
Results may differ from a plain program's by a relative error of at most 0.0003.
Values sent between devices are 32-bit elements; how exact they have to be, the bound alone decides.
A program may use at most 128 MiB of HBM per device.

v0:
```python
import math
import jax
import jax.numpy as jnp
from jax import lax
from jax.sharding import PartitionSpec as P

G = 1024
NBINS = 512
KW = 8
HIGHEST_PRECISION = lax.Precision.HIGHEST


def passed_along(x, axis, by):
    peers = lax.axis_size(axis)
    pairs = [(i, i + by) for i in range(peers) if 0 <= i + by < peers]
    return lax.ppermute(x, axis, pairs)


def look_up_taps(kernel_index, kernel):
    table_rows = kernel.shape[0]
    onehot = (kernel_index[..., None] == jnp.arange(table_rows, dtype=jnp.int32)).astype(
        jnp.float32
    )
    return jnp.einsum("acno,ot->actn", onehot, kernel, precision=HIGHEST_PRECISION)


def visibility_fields(
    visibility, tile_of, u_within, v_cell, kernel_index, kernel, live_count, tile_rows
):
    slots = u_within.shape[1]
    is_live = jnp.arange(slots, dtype=jnp.int32)[None, :] < live_count
    zeroed = jnp.zeros_like(visibility[0])
    real_part = jnp.where(is_live, visibility[0], zeroed)
    imag_part = jnp.where(is_live, visibility[1], zeroed)
    tile_index = tile_of[:, :, 0]
    u_cell = jnp.minimum(tile_index * tile_rows + u_within, G - KW)
    u_cell = u_cell - tile_index * tile_rows
    taps = look_up_taps(kernel_index, kernel)
    fields = jnp.concatenate(
        [
            real_part[:, None],
            imag_part[:, None],
            u_cell[:, None].astype(jnp.float32),
            v_cell[:, None].astype(jnp.float32),
            taps[0],
            taps[1],
        ],
        axis=1,
    )
    return (fields, is_live, tile_index)


def row_taps(fields, row_start, row_count):
    u_cell = fields[2].astype(jnp.int32)
    offset = row_start + jnp.arange(row_count, dtype=jnp.int32)[None, :] - u_cell[:, None]
    taps = jnp.zeros(offset.shape, jnp.float32)
    for tap_index in range(KW):
        taps = taps + jnp.where(offset == tap_index, fields[4 + tap_index][:, None], 0.0)
    return taps


def column_side(fields):
    v_start = fields[3].astype(jnp.int32)
    offset = jnp.arange(G, dtype=jnp.int32)[None, :] - v_start[:, None]
    taps = jnp.zeros(offset.shape, jnp.float32)
    for tap_index in range(KW):
        taps = taps + jnp.where(offset == tap_index, fields[4 + KW + tap_index][:, None], 0.0)
    return jnp.concatenate([fields[0][:, None] * taps, fields[1][:, None] * taps], axis=1)


def contract_slots(upper, lower):
    return lax.dot_general(upper, lower, (((0,), (0,)), ((), ())), precision=HIGHEST_PRECISION)


def grid_rows(fields, row_start, row_count):
    return contract_slots(row_taps(fields, row_start, row_count), column_side(fields))


def dft_matrix():
    positions = jnp.arange(G, dtype=jnp.int32)
    phase = positions[:, None] * positions[None, :] % G
    angle = phase.astype(jnp.float32) * (2.0 * math.pi / G)
    cosine = jnp.cos(angle)
    sine = jnp.sin(angle)
    return jnp.concatenate(
        [jnp.concatenate([cosine, -sine], axis=1), jnp.concatenate([sine, cosine], axis=1)], axis=0
    )


def row_transform(grid_tile, dft_table, tile_rows, channels_here):
    flat_rows = grid_tile.reshape(tile_rows * channels_here, 2 * G)
    halves = jnp.stack(
        [
            jnp.dot(flat_rows, dft_table[:, :G], precision=HIGHEST_PRECISION),
            jnp.dot(flat_rows, dft_table[:, G:], precision=HIGHEST_PRECISION),
        ]
    )
    return halves.reshape(2, tile_rows, channels_here, G)


def to_columns(columns, tile_rows, channels_here):
    return columns.reshape(2 * G, channels_here * tile_rows)


def histogram(stacked, bins):
    row_total = bins.shape[0]
    block_rows = min(64, row_total)
    block_count = row_total // block_rows
    columns = bins.shape[1]
    value_blocks = stacked.reshape(2, block_count, block_rows * columns).transpose(1, 0, 2)
    bin_blocks = bins.reshape(block_count, block_rows * columns)

    def add_block(running, pieces):
        values, bin_ids = pieces
        onehot = (bin_ids[:, None] == jnp.arange(NBINS, dtype=jnp.int32)[None, :]).astype(
            jnp.float32
        )
        return (running + jnp.dot(values, onehot, precision=HIGHEST_PRECISION), None)

    result, _ = lax.scan(add_block, jnp.zeros((2, NBINS), jnp.float32), (value_blocks, bin_blocks))
    return result


def per_device(visibility, tile_of, u_within, v_cell, kernel_index, kernel, live_count, bin_map):
    base_count = lax.axis_size("base")
    freq_count = lax.axis_size("freq")
    tile_rows = G // base_count
    channels_here = visibility.shape[1]
    slots = visibility.shape[2]
    dft_table = dft_matrix()
    fields, is_live, tile_index = visibility_fields(
        visibility, tile_of, u_within, v_cell, kernel_index, kernel, live_count, tile_rows
    )
    capacity = 2 * slots // base_count
    field_count = fields.shape[1]
    chosen = (
        (tile_index[:, :, None] == jnp.arange(base_count, dtype=jnp.int32)[None, None, :])
        & is_live[:, :, None]
    ).astype(jnp.int32)
    before_count = jnp.sum((jnp.cumsum(chosen, axis=1) - chosen) * chosen, axis=2)
    target = jnp.where(is_live, tile_index * capacity + before_count, base_count * capacity)
    outgoing = []
    for channel in range(channels_here):
        placed = (
            jnp.zeros((base_count * capacity, field_count), jnp.float32)
            .at[target[channel]]
            .set(fields[channel].T, mode="drop")
        )
        outgoing.append(placed.reshape(base_count, capacity, field_count).transpose(0, 2, 1))
    received = lax.all_to_all(
        jnp.stack(outgoing, axis=1), "base", split_axis=0, concat_axis=0, tiled=True
    )
    extended = []
    for channel in range(channels_here):
        slot_fields = (
            received[:, channel].transpose(1, 0, 2).reshape(field_count, base_count * capacity)
        )
        extended.append(grid_rows(slot_fields, 0, tile_rows + KW).reshape(tile_rows + KW, 2, G))
    extended = jnp.stack(extended, axis=1)
    incoming = passed_along(extended[tile_rows:], "base", 1)
    grid_tile = extended[:tile_rows].at[:KW].add(incoming)
    halves = row_transform(grid_tile, dft_table, tile_rows, channels_here)
    columns = lax.all_to_all(halves, "base", split_axis=3, concat_axis=1, tiled=True)
    stacked = to_columns(columns, tile_rows, channels_here)
    spectra = contract_slots(dft_table, stacked)
    normalizer = 1.0 / (channels_here * freq_count * slots * base_count)
    squared = spectra[:G] * spectra[:G] + spectra[G:] * spectra[G:]
    power_part = jnp.sum(squared.reshape(G, channels_here, tile_rows), axis=1) * normalizer
    bins_here = bin_map.T
    share_rows = G // freq_count
    share_start = lax.axis_index("freq") * share_rows
    power_share = lax.psum_scatter(power_part, "freq", scatter_dimension=0, tiled=True)
    bins_share = lax.dynamic_slice_in_dim(bins_here, share_start, share_rows, 0)
    bin_sums_local = histogram(jnp.stack([power_share, jnp.ones_like(power_share)]), bins_share)
    totals, counts = lax.psum((bin_sums_local[0], bin_sums_local[1]), ("freq", "base"))
    return (power_share, totals / counts)


def solution(mesh):
    in_specs = (
        P(None, "freq", "base"),
        P("freq", "base", None),
        P("freq", "base"),
        P("freq", "base"),
        P(None, "freq", "base"),
        P(),
        P("freq", "base"),
        P("base", None),
    )
    out_specs = (P("freq", "base"), P())
    return jax.shard_map(
        per_device, mesh=mesh, in_specs=in_specs, out_specs=out_specs, check_vma=False
    )
```

profile of v0, /device:TPU:0, one launch (start us, length us, event | category | flops | bytes accessed | tf_op | source)
XLA Modules:
  0.0 432.0 jit_solution(2849988539622279299)
XLA Ops:
  7.2 0.8 iota_compare_fusion.8
  8.0 0.7 broadcast_compare_fusion
  8.7 0.7 copy.136
  9.4 0.7 fusion.149
  10.1 2.4 reduce-window.6
  13.3 0.8 subtract_convert_fusion
  14.1 0.7 fusion.177
  14.8 1.6 convolution_bitcast_fusion
  16.4 0.7 convert_element_type.75
  17.1 0.7 compare_select_fusion.2
  18.3 1.8 scatter_custom_fusion
  20.5 1.8 scatter_custom_fusion.1
  22.6 0.8 copy.65
  23.4 6.3 %all-to-all-start = ((f32[4,2,20,256]{3,1,2,0:T(2,128)}), f32[4,2,20,256]{3,1,2,0:T(2,128)S(1)}, u32[]{:S(2)}, u32[]{:S(2)}) async-start(f32[4,2,20,256]{3,1,2,0:T(2,128)} %copy.65), calls=%async_computation | async-start | bytes 327680 | tf_op jit(solution)/shard_map/all_to_all | solution.py:150
  29.7 17.5 %fusion.36 = (f32[1024,1024]{1,0:T(8,128)}, f32[1024,1024]{1,0:T(8,128)}) fusion(), kind=kLoop, calls=%fused_computation.59 | loop fusion | flops 14680064 | bytes 8388608 | tf_op jit(solution)/shard_map/sin | solution.py:84
  47.3 16.5 %fusion.38 = f32[1024,1024]{1,0:T(8,128)} fusion(), kind=kLoop, calls=%fused_computation.61 | loop fusion | flops 15728640 | bytes 4194304 | tf_op jit(solution)/shard_map/neg | solution.py:86
  64.2 4.4 %broadcast_multiply_fusion.1 = (f32[1024,1024]{1,0:T(8,128)S(1)}, f32[1024,1024]{1,0:T(8,128)S(1)}) fusion(f32[1024]{0:T(1024)S(1)} %bitcast.240, f32[1024]{0:T(1024)S(1)} %bitcast.258, f32[1024]{0:T(1024)S(1)} %bitcast.256, f32[1024]{0:T(1024)S(1)} %bitcast.254, f32[1024]{0:T(1024)S(1)} %bitcast.252, f32[1024]{0:T(1024)S(1)} %bitcast.250, ...), kind=kLoop, calls=%fused_computation.56 | loop fusion | flops 27262976 | bytes 8433664 | tf_op jit(solution)/shard_map/mul | solution.py:68
  68.6 10.1 %fusion.9 = f32[264,2048]{1,0:T(8,128)} fusion(f32[1024,1024]{1,0:T(8,128)S(1)} %get-tuple-element.127, f32[1024,1024]{1,0:T(8,128)S(1)} %get-tuple-element.126, f32[1024]{0:T(1024)S(1)} %bitcast.276, f32[1024]{0:T(1024)S(1)} %bitcast.274, f32[1024]{0:T(1024)S(1)} %bitcast.272, f32[1024]{0:T(1024)S(1)} %bitcast.270, f32[1024]{0:T(1024)S(1)} %bitcast.284, ...), kind=kOutput, calls=%fused_computation.18 | convolution fusion | flops 6652362752 | bytes 10588160 | tf_op jit(solution)/shard_map/dot_general | solution.py:72
  78.7 3.2 stack_reshape.7
  82.1 4.1 broadcast_multiply_fusion.3
  86.2 10.1 %fusion.5 = f32[264,2048]{1,0:T(8,128)} fusion(f32[1024,1024]{1,0:T(8,128)S(1)} %get-tuple-element.129, f32[1024,1024]{1,0:T(8,128)S(1)} %get-tuple-element.128, f32[1024]{0:T(1024)S(1)} %bitcast.285, f32[1024]{0:T(1024)S(1)} %bitcast.283, f32[1024]{0:T(1024)S(1)} %bitcast.281, f32[1024]{0:T(1024)S(1)} %bitcast.279, f32[1024]{0:T(1024)S(1)} %bitcast.277, ...), kind=kOutput, calls=%fused_computation.14 | convolution fusion | flops 6652362752 | bytes 10588160 | tf_op jit(solution)/shard_map/dot_general | solution.py:72
  96.3 4.1 stack_reshape.6
  100.4 2.5 constant_dynamic-update-slice_fusion.1
  102.9 0.9 constant_dynamic-update-slice_fusion
  103.8 3.9 collective-permute-start
  107.8 12.9 %maximum_maximum_fusion = f32[2048,2048]{1,0:T(8,128)} fusion(f32[1024,1024]{1,0:T(8,128)S(1)} %copy-done.3, f32[1024,1024]{1,0:T(8,128)S(1)} %copy-done.1, f32[1024,1024]{1,0:T(8,128)} %fusion.38), kind=kLoop, calls=%fused_computation.9 | loop fusion | flops 12582912 | bytes 29360128 | tf_op jit(solution)/shard_map/concatenate | solution.py:85
  120.7 3.4 slice.363
  124.1 0.7 fusion.144
  124.8 6.7 %reshape.405 = f32[256,2,2048]{2,0,1:T(8,128)} reshape(f32[256,2,2,1024]{3,2,0,1:T(2,128)} %fusion.144) | data formatting | bytes 8388608 | tf_op jit(solution)/shard_map/reshape.292
  131.5 16.9 %fusion.39 = f32[1,256,2,1024]{3,1,2,0:T(8,128)S(1)} fusion(f32[256,2,2048]{2,0,1:T(8,128)} %reshape.405, f32[2048,2048]{1,0:T(8,128)} %maximum_maximum_fusion), kind=kOutput, calls=%fused_computation.62 | convolution fusion | flops 12884901888 | bytes 14680064 | tf_op jit(solution)/shard_map/dot_general | solution.py:94
  148.4 16.3 %fusion.40 = f32[1,256,2,1024]{3,1,2,0:T(8,128)S(1)} fusion(f32[256,2,2048]{2,0,1:T(8,128)S(1)} %copy-done.5, f32[2048,2048]{1,0:T(8,128)} %maximum_maximum_fusion), kind=kOutput, calls=%fused_computation.63 | convolution fusion | flops 12884901888 | bytes 14680064 | tf_op jit(solution)/shard_map/dot_general | solution.py:95
  164.7 2.3 pad_maximum_fusion
  167.0 7.2 %copy.68 = f32[2,256,2,1024]{1,2,0,3:T(2,128)} copy(f32[2,256,2,1024]{3,1,2,0:T(8,128)} %pad_maximum_fusion) | data formatting | bytes 8388608 | tf_op jit(solution)/shard_map/stack | solution.py:92
  174.2 98.3 %all_to_all.20 = f32[2,256,2,1024]{1,2,0,3:T(2,128)} all-to-all(f32[2,256,2,1024]{1,2,0,3:T(2,128)} %copy.68), channel_id=1, replica_groups=mesh['freq'=8,'base'=4] {'base'}, dimensions={3} | all-to-all | bytes 8388608 | tf_op jit(solution)/shard_map/all_to_all | solution.py:163
  272.5 10.9 %copy.69 = f32[2,256,2,4,256]{4,2,1,3,0:T(2,128)} copy(f32[2,256,2,4,256]{1,2,0,4,3:T(2,128)} %bitcast.228) | data formatting | bytes 8388608 | tf_op jit(solution)/shard_map/all_to_all | solution.py:163
  283.4 4.9 %copy.120 = f32[256,8,2,256]{3,1,2,0:T(8,128)} copy(f32[256,8,2,256]{3,2,1,0:T(2,128)} %bitcast.229) | data formatting | bytes 8388608
  288.3 1.3 copy-done.4
  289.6 33.1 %fusion.175 = f32[2048,512]{0,1:T(8,128)S(1)} fusion(f32[2048,512]{1,0:T(8,128)} %bitcast.231, f32[1024,1024]{1,0:T(8,128)S(1)} %copy-done.4, f32[1024,1024]{1,0:T(8,128)S(1)} %copy-done.2, f32[1024,1024]{1,0:T(8,128)} %fusion.38), kind=kOutput, calls=%fused_computation.257 | convolution fusion | flops 25782386688 | bytes 20971520 | tf_op jit(solution)/shard_map/dot_general | solution.py:72
  323.2 1.2 reduce_sum.19
  324.4 2.3 broadcast_multiply_fusion.4
  327.0 34.9 %reduce-scatter.2.cloned.1.call-done = f32[128,256]{0,1:T(8,128)} async-done(((f32[1024,256]{0,1:T(8,128)}), f32[128,256]{0,1:T(8,128)}) %reduce-scatter.2.cloned.1.call-update) | async-done | bytes 131088 | tf_op jit(solution)/shard_map/reduce_scatter | solution.py:172
  361.9 1.0 copy.79
  363.1 21.1 %while.12 = (s32[]{:T(128)}, f32[2,512]{1,0:T(2,128)S(1)}, f32[2,2,16384]{2,0,1:T(2,128)S(1)}, s32[2,16384]{1,0:T(2,128)S(1)}, s32[]{:T(128)}, /*index=5*/s32[]{:T(128)}) while((s32[]{:T(128)}, f32[2,512]{1,0:T(2,128)S(1)}, f32[2,2,16384]{2,0,1:T(2,128)S(1)}, s32[2,16384]{1,0:T(2,128)S(1)}, s32[]{:T(128)}, ...), condition=%wide.region_8.9_spmd.clone, body=%wide.region_7.8_spmd.clone.sunk | while | flops 209717248 | bytes 598103 | solution.py:120
  363.4 10.3 %fusion.183 = f32[2,512]{1,0:T(2,128)S(1)} fusion(s32[16384]{0:T(1024)S(1)} %bitcast.235, f32[1,2,16384]{2,0,1:T(1,128)S(1)} %constant_dynamic-slice_fusion.5, f32[2,512]{1,0:T(2,128)S(1)} %get-tuple-element.176, pred[]{:T(512)S(6)} %compare.11), kind=kOutput, calls=%fused_computation.5.clone.1 | convolution fusion | flops 209717248 | bytes 204801 | tf_op jit(solution)/shard_map/while/body/eval_jaxpr/dot_general | solution.py:118
  373.9 10.3 %fusion.183 = f32[2,512]{1,0:T(2,128)S(1)} fusion(s32[16384]{0:T(1024)S(1)} %bitcast.235, f32[1,2,16384]{2,0,1:T(1,128)S(1)} %constant_dynamic-slice_fusion.5, f32[2,512]{1,0:T(2,128)S(1)} %get-tuple-element.176, pred[]{:T(512)S(6)} %compare.11), kind=kOutput, calls=%fused_computation.5.clone.1 | convolution fusion | flops 209717248 | bytes 204801 | tf_op jit(solution)/shard_map/while/body/eval_jaxpr/dot_general | solution.py:118
  384.2 39.3 %all-reduce.1 = (f32[512]{0:T(512)S(1)}, f32[512]{0:T(512)S(1)}) all-reduce(f32[512]{0:T(512)S(1)} %bitcast.265, f32[512]{0:T(512)S(1)} %bitcast.264), channel_id=1, replica_groups=mesh['freq'=8,'base'=4] {'freq','base'}, use_global_device_ids=true, to_apply=%region_9.10 | all-reduce | flops 1024 | bytes 8192 | tf_op jit(solution)/shard_map/psum | solution.py:175
  423.5 0.6 div.3
  424.1 0.8 copy.73
  (93 shorter events, 3.5 us)
Async XLA Ops:
  7.2 319.6 %copy-start = (s32[256,1024]{1,0:T(8,128)S(1)}, s32[256,1024]{1,0:T(8,128)}, u32[]{:S(2)}) copy-start(s32[256,1024]{1,0:T(8,128)} %param.19) | copy-start | bytes 3145732
  23.4 40.4 %all-to-all-start = ((f32[4,2,20,256]{3,1,2,0:T(2,128)}), f32[4,2,20,256]{3,1,2,0:T(2,128)S(1)}, u32[]{:S(2)}, u32[]{:S(2)}) async-start(f32[4,2,20,256]{3,1,2,0:T(2,128)} %copy.65), calls=%async_computation | async-start | bytes 327680 | tf_op jit(solution)/shard_map/all_to_all | solution.py:150
  29.7 332.2 %reduce-scatter.2.cloned.1.call-start = ((), (), s32[]{:S(2)}) async-start(), calls=%async_computation.3 | async-start | bytes 1179648 | tf_op jit(solution)/shard_map/reduce_scatter | solution.py:172
  100.4 7.4 %copy-start.1 = (f32[1024,1024]{1,0:T(8,128)S(1)}, f32[1024,1024]{1,0:T(8,128)}, u32[]{:S(2)}) copy-start(f32[1024,1024]{1,0:T(8,128)} %get-tuple-element.142) | copy-start | bytes 12582916
  100.4 7.4 %copy-start.3 = (f32[1024,1024]{1,0:T(8,128)S(1)}, f32[1024,1024]{1,0:T(8,128)}, u32[]{:S(2)}) copy-start(f32[1024,1024]{1,0:T(8,128)} %get-tuple-element.143) | copy-start | bytes 12582916
  103.8 20.3 %collective-permute-start = (f32[8,2,2,1024]{3,2,0,1:T(2,128)S(1)}, f32[8,2,2,1024]{3,2,0,1:T(2,128)S(1)}, u32[]{:S(2)}, u32[]{:S(2)}) collective-permute-start(f32[8,2,2,1024]{3,2,0,1:T(2,128)S(1)} %slice.365), channel_id=1, source_target_pairs={{0,1},{1,2},{2,3},{4,5},{5,6},{6,7},{8,9},{9,10},{10,11},{12,13},{... | collective-permute-start | bytes 393224 | tf_op jit(solution)/shard_map/ppermute | solution.py:16
  131.5 16.9 %copy-start.5 = (f32[256,2,2048]{2,0,1:T(8,128)S(1)}, f32[256,2,2048]{2,0,1:T(8,128)}, u32[]{:S(2)}) copy-start(f32[256,2,2048]{2,0,1:T(8,128)} %reshape.405) | copy-start | bytes 12582916
  283.4 4.9 %copy-start.2 = (f32[1024,1024]{1,0:T(8,128)S(1)}, f32[1024,1024]{1,0:T(8,128)}, u32[]{:S(2)}) copy-start(f32[1024,1024]{1,0:T(8,128)} %get-tuple-element.142) | copy-start | bytes 12582916
  283.4 6.2 %copy-start.4 = (f32[1024,1024]{1,0:T(8,128)S(1)}, f32[1024,1024]{1,0:T(8,128)}, u32[]{:S(2)}) copy-start(f32[1024,1024]{1,0:T(8,128)} %get-tuple-element.143) | copy-start | bytes 12582916
  363.1 61.0 %copy-start.6 = (f32[128,256]{0,1:T(8,128)S(1)}, f32[128,256]{0,1:T(8,128)}, u32[]{:S(2)}) copy-start(f32[128,256]{0,1:T(8,128)} %reduce-scatter.2.cloned.1.call-done) | copy-start | bytes 393220
Sparse Core Ops, SparseCore 0:
  326.8 35.0 reduce-scatter.1
where the time goes:
time: 440 us; the launch traced here: 432 us
  blocking collectives  138 us (31%)
  matrix products  109 us (25%)
  other arithmetic  70.4 us (16%)
  local copies, waits for them, and re-layouts  55.1 us (13%)
  waiting for transfers between devices  35 us (8%)
  between operations  14.9 us (3%)
  starting transfers between devices  10.3 us (2%)
    all_to_all x1, blocking collectives, per_device(): lax.all_to_all(halves, 'base', split_axis=3, concat_axis=1, tiled=True)  98.3 us
    dot_general x3, matrix products, contract_slots(): lax.dot_general(upper, lower, (((0,), (0,)), ((), ())), precision=HIGHEST...  53.3 us
    psum x1, blocking collectives, per_device(): lax.psum((bin_sums_local[0], bin_sums_local[1]), ('freq', 'base'))  39.3 us
    reduce_scatter x1, waiting for transfers between devices, per_device(): lax.psum_scatter(power_part, 'freq', scatter_dimension=0, tiled=True)  34.9 us
    dot_general x2, matrix products, add_block(): jnp.dot(values, onehot, precision=HIGHEST_PRECISION)  20.6 us
    sin x1, other arithmetic, dft_matrix(): sine = jnp.sin(angle)  17.5 us
    dot_general x1, matrix products, row_transform(): jnp.dot(flat_rows, dft_table[:, :G], precision=HIGHEST_PRECISION)  16.9 us
    neg x1, other arithmetic, dft_matrix(): -sine  16.5 us
  transfers between devices with their start and end apart: 3, of which 1 were waited for; matrix products, arithmetic and copies ran while one was open for 12% of the time, Pallas kernels for 0%

commit v1 on v0

--- a/solution.py
+++ b/solution.py
@@ -3,6 +3,7 @@
 import jax.numpy as jnp
 from jax import lax
 from jax.sharding import PartitionSpec as P
+from jax.lax import all_to_all, axis_size
 
 G = 1024
 NBINS = 512
@@ -160,7 +161,15 @@
     incoming = passed_along(extended[tile_rows:], "base", 1)
     grid_tile = extended[:tile_rows].at[:KW].add(incoming)
     halves = row_transform(grid_tile, dft_table, tile_rows, channels_here)
-    columns = lax.all_to_all(halves, "base", split_axis=3, concat_axis=1, tiled=True)
+    columns = jnp.concatenate(
+        all_to_all(
+            jnp.stack(jnp.split(halves, axis_size("base"), axis=3), 0),
+            split_axis=0,
+            axis_name="base",
+            concat_axis=0,
+        ),
+        1,
+    )
     stacked = to_columns(columns, tile_rows, channels_here)
     spectra = contract_slots(dft_table, stacked)
     normalizer = 1.0 / (channels_here * freq_count * slots * base_count)

time: 440 us -> 425 us (0.966)
  local copies, waits for them, and re-layouts: 55.1 us -> 42.1 us
    all_to_all x1 -> x0, local copies, waits for them, and re-layouts: 10.9 us -> none  [per_device(): lax.all_to_all(halves, 'base', split_axis=3, concat_axis=1, tiled=True)]
    another operation x4 -> x3, local copies, waits for them, and re-layouts: 14.2 us -> 6.96 us  [the longest x1 7.22 us: row_transform(): jnp.stack([jnp.dot(flat_rows, dft_table[:, :G], precision=HIGHEST_PRECISI...]
    reshape x0 -> x1, local copies, waits for them, and re-layouts: none -> 5.21 us  [per_device(): jnp.concatenate(all_to_all(jnp.stack(jnp.split(halves, axis_size('base'),...]
    unnamed x61 -> x63, local copies, waits for them, and re-layouts: 11.4 us -> 11.4 us
where the time goes in v1:
time: 425 us; the launch traced here: 417 us
  blocking collectives  135 us (32%)
  matrix products  109 us (26%)
  other arithmetic  70.9 us (17%)
  local copies, waits for them, and re-layouts  42.1 us (10%)
  waiting for transfers between devices  35 us (8%)
  between operations  14.9 us (4%)
  starting transfers between devices  10.3 us (2%)
    all_to_all x1, blocking collectives, per_device(): all_to_all(jnp.stack(jnp.split(halves, axis_size('base'), axis=3), 0), sp...  95.7 us
    dot_general x3, matrix products, contract_slots(): lax.dot_general(upper, lower, (((0,), (0,)), ((), ())), precision=HIGHEST...  53.6 us
    psum x1, blocking collectives, per_device(): lax.psum((bin_sums_local[0], bin_sums_local[1]), ('freq', 'base'))  39.3 us
    reduce_scatter x1, waiting for transfers between devices, per_device(): lax.psum_scatter(power_part, 'freq', scatter_dimension=0, tiled=True)  35 us
    dot_general x2, matrix products, add_block(): jnp.dot(values, onehot, precision=HIGHEST_PRECISION)  20.6 us
    sin x1, other arithmetic, dft_matrix(): sine = jnp.sin(angle)  17.6 us
    dot_general x1, matrix products, row_transform(): jnp.dot(flat_rows, dft_table[:, G:], precision=HIGHEST_PRECISION)  16.9 us
    dot_general x1, matrix products, row_transform(): jnp.dot(flat_rows, dft_table[:, :G], precision=HIGHEST_PRECISION)  16.5 us
  transfers between devices with their start and end apart: 3, of which 1 were waited for; matrix products, arithmetic and copies ran while one was open for 12% of the time, Pallas kernels for 0%

profile of v1, /device:TPU:0, one launch (start us, length us, event | category | flops | bytes accessed | tf_op | source)
XLA Modules:
  0.0 417.5 jit_solution(17929528038494484764)
XLA Ops:
  7.2 0.8 iota_compare_fusion.8
  8.0 0.7 broadcast_compare_fusion
  8.7 0.7 copy.132
  9.4 0.7 fusion.156
  10.1 2.4 reduce-window.6
  13.3 0.8 subtract_convert_fusion
  14.1 0.7 fusion.184
  14.8 1.6 convolution_bitcast_fusion
  16.4 0.7 convert_element_type.75
  17.1 0.7 compare_select_fusion.2
  18.3 1.8 scatter_custom_fusion
  20.5 1.8 scatter_custom_fusion.1
  22.6 0.8 copy.62
  23.4 6.3 %all-to-all-start = ((f32[4,2,20,256]{3,1,2,0:T(2,128)}), f32[4,2,20,256]{3,1,2,0:T(2,128)S(1)}, u32[]{:S(2)}, u32[]{:S(2)}) async-start(f32[4,2,20,256]{3,1,2,0:T(2,128)} %copy.62), calls=%async_computation | async-start | bytes 327680 | tf_op jit(solution)/shard_map/all_to_all | solution.py:151
  29.7 17.6 %fusion.36 = (f32[1024,1024]{1,0:T(8,128)}, f32[1024,1024]{1,0:T(8,128)}) fusion(), kind=kLoop, calls=%fused_computation.65 | loop fusion | flops 14680064 | bytes 8388608 | tf_op jit(solution)/shard_map/sin | solution.py:85
  47.3 16.5 %fusion.38 = f32[1024,1024]{1,0:T(8,128)} fusion(), kind=kLoop, calls=%fused_computation.67 | loop fusion | flops 15728640 | bytes 4194304 | tf_op jit(solution)/shard_map/neg | solution.py:87
  64.2 4.1 broadcast_multiply_fusion.1
  68.3 10.1 %fusion.9 = f32[264,2048]{1,0:T(8,128)} fusion(f32[1024,1024]{1,0:T(8,128)S(1)} %get-tuple-element.131, f32[1024,1024]{1,0:T(8,128)S(1)} %get-tuple-element.130, f32[1024]{0:T(1024)S(1)} %bitcast.287, f32[1024]{0:T(1024)S(1)} %bitcast.285, f32[1024]{0:T(1024)S(1)} %bitcast.283, f32[1024]{0:T(1024)S(1)} %bitcast.281, f32[1024]{0:T(1024)S(1)} %bitcast.279, ...), kind=kOutput, calls=%fused_computation.18 | convolution fusion | flops 6652362752 | bytes 10588160 | tf_op jit(solution)/shard_map/dot_general | solution.py:73
  78.4 3.2 stack_reshape.7
  81.8 4.1 broadcast_multiply_fusion.3
  86.0 10.1 %fusion.5 = f32[264,2048]{1,0:T(8,128)} fusion(f32[1024,1024]{1,0:T(8,128)S(1)} %get-tuple-element.133, f32[1024,1024]{1,0:T(8,128)S(1)} %get-tuple-element.132, f32[1024]{0:T(1024)S(1)} %bitcast.292, f32[1024]{0:T(1024)S(1)} %bitcast.290, f32[1024]{0:T(1024)S(1)} %bitcast.288, f32[1024]{0:T(1024)S(1)} %bitcast.286, f32[1024]{0:T(1024)S(1)} %bitcast.284, ...), kind=kOutput, calls=%fused_computation.14 | convolution fusion | flops 6652362752 | bytes 10588160 | tf_op jit(solution)/shard_map/dot_general | solution.py:73
  96.1 4.1 stack_reshape.6
  100.2 2.5 constant_dynamic-update-slice_fusion.1
  102.7 0.9 constant_dynamic-update-slice_fusion
  103.6 3.9 collective-permute-start
  107.5 12.8 %maximum_maximum_fusion = f32[2048,2048]{1,0:T(8,128)} fusion(f32[1024,1024]{1,0:T(8,128)S(1)} %copy-done.3, f32[1024,1024]{1,0:T(8,128)S(1)} %copy-done.1, f32[1024,1024]{1,0:T(8,128)} %fusion.38), kind=kLoop, calls=%fused_computation.9 | loop fusion | flops 12582912 | bytes 29360128 | tf_op jit(solution)/shard_map/concatenate | solution.py:86
  120.4 3.4 slice.363
  123.7 0.8 fusion.151
  124.5 6.7 %reshape.404 = f32[256,2,2048]{2,0,1:T(8,128)} reshape(f32[256,2,2,1024]{3,2,0,1:T(2,128)} %fusion.151) | data formatting | bytes 8388608 | tf_op jit(solution)/shard_map/reshape.291
  131.2 16.9 %fusion.40 = f32[1,256,2,1024]{3,1,2,0:T(8,128)S(1)} fusion(f32[256,2,2048]{2,0,1:T(8,128)} %reshape.404, f32[2048,2048]{1,0:T(8,128)} %maximum_maximum_fusion), kind=kOutput, calls=%fused_computation.69 | convolution fusion | flops 12884901888 | bytes 14680064 | tf_op jit(solution)/shard_map/dot_general | solution.py:96
  148.1 16.5 %fusion.39 = f32[1,256,2,1024]{3,1,2,0:T(8,128)S(1)} fusion(f32[256,2,2048]{2,0,1:T(8,128)S(1)} %copy-done.6, f32[2048,2048]{1,0:T(8,128)} %maximum_maximum_fusion), kind=kOutput, calls=%fused_computation.68 | convolution fusion | flops 12884901888 | bytes 14680064 | tf_op jit(solution)/shard_map/dot_general | solution.py:95
  164.6 0.5 fusion.106
  165.4 95.7 %all_to_all.10 = f32[4,2,256,2,256]{4,2,3,1,0:T(8,128)S(1)} all-to-all(f32[4,2,256,2,256]{4,2,3,1,0:T(8,128)S(1)} %pad_maximum_fusion), channel_id=1, replica_groups=mesh['freq'=8,'base'=4] {'base'}, dimensions={0} | all-to-all | bytes 8388608 | tf_op jit(solution)/shard_map/all_to_all | solution.py:165
  261.1 5.2 %copy.65 = f32[2,4,256,2,256]{4,3,2,1,0:T(2,128)} copy(f32[2,4,256,2,256]{4,2,3,0,1:T(8,128)S(1)} %bitcast.235) | data formatting | bytes 8388608 | tf_op jit(solution)/shard_map/reshape | solution.py:164
  266.4 4.9 %copy.116 = f32[256,8,2,256]{3,1,2,0:T(8,128)} copy(f32[256,8,2,256]{3,2,1,0:T(2,128)} %bitcast.236) | data formatting | bytes 8388608
  271.3 1.3 copy-done.4
  272.6 33.4 %fusion.182 = f32[2048,512]{0,1:T(8,128)} fusion(f32[2048,512]{1,0:T(8,128)} %bitcast.238, f32[1024,1024]{1,0:T(8,128)S(1)} %copy-done.4, f32[1024,1024]{1,0:T(8,128)S(1)} %copy-done.2, f32[1024,1024]{1,0:T(8,128)S(1)} %copy-done.5), kind=kOutput, calls=%fused_computation.271 | convolution fusion | flops 25782386688 | bytes 20971520 | tf_op jit(solution)/shard_map/dot_general | solution.py:73
  306.0 2.7 fusion.35
  308.7 1.2 reduce_sum.19
  309.9 2.3 broadcast_multiply_fusion.4
  312.5 35.0 %reduce-scatter.2.cloned.1.call-done = f32[128,256]{0,1:T(8,128)} async-done(((f32[1024,256]{0,1:T(8,128)}), f32[128,256]{0,1:T(8,128)}) %reduce-scatter.2.cloned.1.call-update) | async-done | bytes 131088 | tf_op jit(solution)/shard_map/reduce_scatter | solution.py:181
  347.5 1.0 copy.75
  348.8 21.1 %while.12 = (s32[]{:T(128)}, f32[2,512]{1,0:T(2,128)S(1)}, f32[2,2,16384]{2,0,1:T(2,128)S(1)}, s32[2,16384]{1,0:T(2,128)S(1)}, s32[]{:T(128)}, /*index=5*/s32[]{:T(128)}) while((s32[]{:T(128)}, f32[2,512]{1,0:T(2,128)S(1)}, f32[2,2,16384]{2,0,1:T(2,128)S(1)}, s32[2,16384]{1,0:T(2,128)S(1)}, s32[]{:T(128)}, ...), condition=%wide.region_8.9_spmd.clone, body=%wide.region_7.8_spmd.clone.sunk | while | flops 209717248 | bytes 598103 | solution.py:121
  349.0 10.3 %fusion.190 = f32[2,512]{1,0:T(2,128)S(1)} fusion(s32[16384]{0:T(1024)S(1)} %bitcast.242, f32[1,2,16384]{2,0,1:T(1,128)S(1)} %constant_dynamic-slice_fusion.5, f32[2,512]{1,0:T(2,128)S(1)} %get-tuple-element.180, pred[]{:T(512)S(6)} %compare.11), kind=kOutput, calls=%fused_computation.5.clone.1 | convolution fusion | flops 209717248 | bytes 204801 | tf_op jit(solution)/shard_map/while/body/eval_jaxpr/dot_general | solution.py:119
  359.5 10.3 %fusion.190 = f32[2,512]{1,0:T(2,128)S(1)} fusion(s32[16384]{0:T(1024)S(1)} %bitcast.242, f32[1,2,16384]{2,0,1:T(1,128)S(1)} %constant_dynamic-slice_fusion.5, f32[2,512]{1,0:T(2,128)S(1)} %get-tuple-element.180, pred[]{:T(512)S(6)} %compare.11), kind=kOutput, calls=%fused_computation.5.clone.1 | convolution fusion | flops 209717248 | bytes 204801 | tf_op jit(solution)/shard_map/while/body/eval_jaxpr/dot_general | solution.py:119
  369.9 39.3 %all-reduce.1 = (f32[512]{0:T(512)S(1)}, f32[512]{0:T(512)S(1)}) all-reduce(f32[512]{0:T(512)S(1)} %bitcast.272, f32[512]{0:T(512)S(1)} %bitcast.271), channel_id=1, replica_groups=mesh['freq'=8,'base'=4] {'freq','base'}, use_global_device_ids=true, to_apply=%region_9.10 | all-reduce | flops 1024 | bytes 8192 | tf_op jit(solution)/shard_map/psum | solution.py:184
  409.1 0.6 div.3
  409.7 0.8 copy.69
  (95 shorter events, 3.4 us)
Async XLA Ops:
  7.2 305.1 %copy-start = (s32[256,1024]{1,0:T(8,128)S(1)}, s32[256,1024]{1,0:T(8,128)}, u32[]{:S(2)}) copy-start(s32[256,1024]{1,0:T(8,128)} %param.19) | copy-start | bytes 3145732
  23.4 40.4 %all-to-all-start = ((f32[4,2,20,256]{3,1,2,0:T(2,128)}), f32[4,2,20,256]{3,1,2,0:T(2,128)S(1)}, u32[]{:S(2)}, u32[]{:S(2)}) async-start(f32[4,2,20,256]{3,1,2,0:T(2,128)} %copy.62), calls=%async_computation | async-start | bytes 327680 | tf_op jit(solution)/shard_map/all_to_all | solution.py:151
  29.7 317.8 %reduce-scatter.2.cloned.1.call-start = ((), (), s32[]{:S(2)}) async-start(), calls=%async_computation.3 | async-start | bytes 1179648 | tf_op jit(solution)/shard_map/reduce_scatter | solution.py:181
  100.2 7.4 %copy-start.1 = (f32[1024,1024]{1,0:T(8,128)S(1)}, f32[1024,1024]{1,0:T(8,128)}, u32[]{:S(2)}) copy-start(f32[1024,1024]{1,0:T(8,128)} %get-tuple-element.146) | copy-start | bytes 12582916
  100.2 7.4 %copy-start.3 = (f32[1024,1024]{1,0:T(8,128)S(1)}, f32[1024,1024]{1,0:T(8,128)}, u32[]{:S(2)}) copy-start(f32[1024,1024]{1,0:T(8,128)} %get-tuple-element.147) | copy-start | bytes 12582916
  103.6 20.2 %collective-permute-start = (f32[8,2,2,1024]{3,2,0,1:T(2,128)S(1)}, f32[8,2,2,1024]{3,2,0,1:T(2,128)S(1)}, u32[]{:S(2)}, u32[]{:S(2)}) collective-permute-start(f32[8,2,2,1024]{3,2,0,1:T(2,128)S(1)} %slice.365), channel_id=1, source_target_pairs={{0,1},{1,2},{2,3},{4,5},{5,6},{6,7},{8,9},{9,10},{10,11},{12,13},{... | collective-permute-start | bytes 393224 | tf_op jit(solution)/shard_map/ppermute | solution.py:17
  131.2 16.9 %copy-start.6 = (f32[256,2,2048]{2,0,1:T(8,128)S(1)}, f32[256,2,2048]{2,0,1:T(8,128)}, u32[]{:S(2)}) copy-start(f32[256,2,2048]{2,0,1:T(8,128)} %reshape.404) | copy-start | bytes 12582916
  261.1 10.2 %copy-start.5 = (f32[1024,1024]{1,0:T(8,128)S(1)}, f32[1024,1024]{1,0:T(8,128)}, u32[]{:S(2)}) copy-start(f32[1024,1024]{1,0:T(8,128)} %fusion.38) | copy-start | bytes 12582916
  266.3 4.9 %copy-start.2 = (f32[1024,1024]{1,0:T(8,128)S(1)}, f32[1024,1024]{1,0:T(8,128)}, u32[]{:S(2)}) copy-start(f32[1024,1024]{1,0:T(8,128)} %get-tuple-element.146) | copy-start | bytes 12582916
  266.4 6.2 %copy-start.4 = (f32[1024,1024]{1,0:T(8,128)S(1)}, f32[1024,1024]{1,0:T(8,128)}, u32[]{:S(2)}) copy-start(f32[1024,1024]{1,0:T(8,128)} %get-tuple-element.147) | copy-start | bytes 12582916
  348.8 61.0 %copy-start.7 = (f32[128,256]{0,1:T(8,128)S(1)}, f32[128,256]{0,1:T(8,128)}, u32[]{:S(2)}) copy-start(f32[128,256]{0,1:T(8,128)} %reduce-scatter.2.cloned.1.call-done) | copy-start | bytes 393220
Sparse Core Ops, SparseCore 0:
  312.4 35.1 reduce-scatter.1
